TPU v7x, 32 devices: a whole 2x2x4 slice. The times are simulated.
32 devices in a mesh: pair: 4 (over x, core), row: 8 (over z, y).
Axes of the slice: x: 2, y: 2, z: 4, core: 2. Of those that a mesh axis runs over, the one named last changes fastest.
Arguments:
- descriptors: bfloat16 [32, 2048, 256], P('pair', 'row'), parts along dimension 0, may hold values from -8 to 8
- counts: int32 [32], P('pair'), parts along dimension 0, may hold values from 512 to 2048
- pairs: int32 [16, 2], P('pair'), parts along dimension 0, may hold values from 0 to 7, as said below
- bin_score: float32 [1], replicated, may hold values from 0.5 to 2
Outputs:
- log_match: float32 [16, 2048, 2048], P('pair', 'row'), parts along dimension 0
- row_bins: float32 [16, 2048], P('pair', 'row'), parts along dimension 0
- col_bins: float32 [16, 2048], P('pair'), parts along dimension 0
There are 4 independent parts, one for each index of `pair`. A program takes and returns all parts, laid end to end along the dimension named above; an argument that names none is the same for every part. Nothing has to cross between parts.
Inputs may be any that keep to these rules, and one draw needn't show every extreme that they name: Image k's keypoints are its first counts[k] slots. `pairs`: the two images of a pair differ.
All inputs are finite; a program needn't handle non-finite values.
Results may differ from a plain program's by a relative error of at most 0.0003.
Values may be sent and summed in bfloat16 or wider, within the bound.
A program may use at most 64 MiB of HBM per device.

v0:
```python
import jax
import jax.numpy as jnp
from jax import lax
from jax.sharding import PartitionSpec as P

D = 256
ITERS = 10


NEG = -1e30


def finish(peaks, totals, bin_extra):
    ceiling = jnp.maximum(peaks, bin_extra)
    return ceiling + jnp.log(totals * jnp.exp(peaks - ceiling) + jnp.exp(bin_extra - ceiling))


def local_stats(shifted, kept, reduce_dim):
    peaks = jnp.max(shifted, axis=reduce_dim)
    totals = jnp.sum(
        jnp.where(kept, jnp.exp(shifted - jnp.expand_dims(peaks, reduce_dim)), 0.0), axis=reduce_dim
    )
    return (peaks, totals)


def on_device(descriptors, counts, pairs, bin_score):
    local_rows = descriptors.shape[1]
    all_cols = local_rows * lax.axis_size("row")
    score_scale = D ** (-0.5)
    offset = lax.axis_index("row") * local_rows
    row_desc = descriptors[pairs[:, 0]]
    col_desc = descriptors[pairs[:, 1]]
    n_rows = counts[pairs[:, 0]]
    n_cols = counts[pairs[:, 1]]
    bin_value = bin_score[0]
    scores = (
        jnp.einsum(
            "prd,pcd->prc",
            row_desc,
            lax.all_gather(col_desc, "row", axis=1, tiled=True),
            preferred_element_type=jnp.float32,
        )
        * score_scale
    )
    row_index = offset + lax.iota(jnp.int32, local_rows)
    row_kept = row_index[None, :] < n_rows[:, None]
    col_kept = lax.iota(jnp.int32, all_cols)[None, :] < n_cols[:, None]
    row_count = n_rows.astype(jnp.float32)
    col_count = n_cols.astype(jnp.float32)
    log_norm = -jnp.log(row_count + col_count)
    mu_bin = jnp.log(col_count) + log_norm
    nu_bin = jnp.log(row_count) + log_norm

    def row_pass(col_pot, col_bin):
        shifted = jnp.where(col_kept[:, None, :], scores + col_pot[:, None, :], NEG)
        bin_edge = bin_value + col_bin
        peaks, totals = local_stats(shifted, col_kept[:, None, :], 2)
        row_pot = log_norm[:, None] - finish(peaks, totals, bin_edge[:, None])
        bin_line = jnp.where(col_kept, bin_value + col_pot, NEG)
        bin_peak, bin_total = local_stats(bin_line, col_kept, 1)
        row_bin = mu_bin - finish(bin_peak, bin_total, bin_edge)
        return (row_pot, row_bin)

    def column_pass(row_pot, row_bin):
        shifted = jnp.where(row_kept[:, :, None], scores + row_pot[:, :, None], NEG)
        edge_rows = jnp.where(row_kept, bin_value + row_pot, NEG)
        bin_extra = bin_value + row_bin
        peaks, bin_peak = (
            lax.pmax(jnp.max(shifted, axis=1).astype(jnp.bfloat16), "row").astype(jnp.float32),
            lax.pmax(jnp.max(edge_rows, axis=1).astype(jnp.bfloat16), "row").astype(jnp.float32),
        )
        totals = jnp.sum(
            jnp.where(row_kept[:, :, None], jnp.exp(shifted - peaks[:, None, :]), 0.0), axis=1
        )
        bin_total = jnp.sum(
            jnp.where(row_kept, jnp.exp(edge_rows - bin_peak[:, None]), 0.0), axis=1
        )
        totals, bin_total = lax.psum((totals, bin_total), "row")
        col_pot = log_norm[:, None] - finish(peaks, totals, bin_extra[:, None])
        col_bin = nu_bin - finish(bin_peak, bin_total, bin_extra)
        return (col_pot, col_bin)

    def sweep(sweep_index, carried):
        row_pot, row_bin = row_pass(carried[0], carried[1])
        col_pot, col_bin = column_pass(row_pot, row_bin)
        return (col_pot, col_bin, row_pot, row_bin)

    pair_count = scores.shape[0]
    initial = (
        jnp.zeros((pair_count, all_cols), jnp.float32),
        jnp.zeros((pair_count,), jnp.float32),
        jnp.zeros((pair_count, local_rows), jnp.float32),
        jnp.zeros((pair_count,), jnp.float32),
    )
    col_pot, col_bin, row_pot, row_bin = lax.fori_loop(0, ITERS, sweep, initial)
    both_kept = row_kept[:, :, None] & col_kept[:, None, :]
    log_match = jnp.where(
        both_kept, scores + row_pot[:, :, None] + col_pot[:, None, :] - log_norm[:, None, None], 0.0
    )
    row_bins = jnp.where(row_kept, bin_value + row_pot + col_bin[:, None] - log_norm[:, None], 0.0)
    col_bins = jnp.where(col_kept, bin_value + row_bin[:, None] + col_pot - log_norm[:, None], 0.0)
    return (log_match, row_bins, col_bins)


def solution(mesh):
    return jax.shard_map(
        on_device,
        mesh=mesh,
        in_specs=(P("pair", "row", None), P("pair"), P("pair", None), P()),
        out_specs=(P("pair", "row", None), P("pair", "row"), P("pair", None)),
        check_vma=False,
    )
```

profile of v0, /device:TPU:0, one launch (start us, length us, event | category | flops | bytes accessed | tf_op | source)
XLA Modules:
  0.0 975.9 jit_solution(7637766511083870243)
XLA Ops:
  13.8 72.5 %all-gather.3.cloned.1.call-done = bf16[4,2048,256]{2,1,0:T(8,128)(2,1)} async-done(((bf16[4,256,256]{2,1,0:T(8,128)(2,1)}), bf16[4,2048,256]{2,1,0:T(8,128)(2,1)}) %all-gather.3.cloned.1.call-update) | async-done | bytes 4194320 | tf_op jit(solution)/shard_map/all_gather | solution.py:40
  86.3 6.9 convolution_multiply_fusion
  93.1 866.7 %while.18 = (s32[]{:T(128)}, f32[4,2048]{1,0:T(4,128)S(1)}, f32[4]{0:T(128)S(1)}, f32[4,256]{1,0:T(4,128)}, f32[4]{0:T(128)}, /*index=5*/f32[4]{0:T(128)S(1)}, f...) while((s32[]{:T(128)}, f32[4,2048]{1,0:T(4,128)S(1)}, ...), condition=%wide.region_13.14_spmd.clone.clone, body=%wide.region_0.13_spmd.clone.sunk.clone | while | flops 33740880 | bytes 67667624 | solution.py:95
  103.8 34.7 %all-reduce.6 = (bf16[4,2048]{1,0:T(4,128)(2,1)S(1)}, bf16[4]{0:T(256)(128)(2,1)S(1)}) all-reduce(bf16[4,2048]{1,0:T(4,128)(2,1)S(1)} %fusion.46, bf16[4]{0:T(256)(128)(2,1)S(1)} %get-tuple-element.276), channel_id=1, replica_groups=mesh['pair'=4,'row'=8] {'row'}, use_global_device_ids=true, to_apply=%region_4.4 | all-reduce | flops 8196 | bytes 32784 | tf_op jit(solution)/shard_map/while/body/eval_jaxpr/pmax | solution.py:69
  139.4 4.8 select_reduce_fusion.13
  144.1 33.4 %all-reduce.7 = (f32[4,2048]{1,0:T(4,128)S(1)}, f32[4]{0:T(128)S(1)}) all-reduce(f32[4,2048]{1,0:T(4,128)S(1)} %select_reduce_fusion.13, f32[4]{0:T(128)S(1)} %select_reduce_fusion.14), channel_id=1, replica_groups=mesh['pair'=4,'row'=8] {'row'}, use_global_device_ids=true, to_apply=%region_8.8 | all-reduce | flops 8196 | bytes 65568 | tf_op jit(solution)/shard_map/while/body/eval_jaxpr/psum | solution.py:78
  190.3 34.9 %all-reduce.6 = (bf16[4,2048]{1,0:T(4,128)(2,1)S(1)}, bf16[4]{0:T(256)(128)(2,1)S(1)}) all-reduce(bf16[4,2048]{1,0:T(4,128)(2,1)S(1)} %fusion.46, bf16[4]{0:T(256)(128)(2,1)S(1)} %get-tuple-element.276), channel_id=1, replica_groups=mesh['pair'=4,'row'=8] {'row'}, use_global_device_ids=true, to_apply=%region_4.4 | all-reduce | flops 8196 | bytes 32784 | tf_op jit(solution)/shard_map/while/body/eval_jaxpr/pmax | solution.py:69
  226.1 4.8 select_reduce_fusion.13
  230.9 33.3 %all-reduce.7 = (f32[4,2048]{1,0:T(4,128)S(1)}, f32[4]{0:T(128)S(1)}) all-reduce(f32[4,2048]{1,0:T(4,128)S(1)} %select_reduce_fusion.13, f32[4]{0:T(128)S(1)} %select_reduce_fusion.14), channel_id=1, replica_groups=mesh['pair'=4,'row'=8] {'row'}, use_global_device_ids=true, to_apply=%region_8.8 | all-reduce | flops 8196 | bytes 65568 | tf_op jit(solution)/shard_map/while/body/eval_jaxpr/psum | solution.py:78
  277.0 34.9 %all-reduce.6 = (bf16[4,2048]{1,0:T(4,128)(2,1)S(1)}, bf16[4]{0:T(256)(128)(2,1)S(1)}) all-reduce(bf16[4,2048]{1,0:T(4,128)(2,1)S(1)} %fusion.46, bf16[4]{0:T(256)(128)(2,1)S(1)} %get-tuple-element.276), channel_id=1, replica_groups=mesh['pair'=4,'row'=8] {'row'}, use_global_device_ids=true, to_apply=%region_4.4 | all-reduce | flops 8196 | bytes 32784 | tf_op jit(solution)/shard_map/while/body/eval_jaxpr/pmax | solution.py:69
  312.7 4.8 select_reduce_fusion.13
  317.5 33.3 %all-reduce.7 = (f32[4,2048]{1,0:T(4,128)S(1)}, f32[4]{0:T(128)S(1)}) all-reduce(f32[4,2048]{1,0:T(4,128)S(1)} %select_reduce_fusion.13, f32[4]{0:T(128)S(1)} %select_reduce_fusion.14), channel_id=1, replica_groups=mesh['pair'=4,'row'=8] {'row'}, use_global_device_ids=true, to_apply=%region_8.8 | all-reduce | flops 8196 | bytes 65568 | tf_op jit(solution)/shard_map/while/body/eval_jaxpr/psum | solution.py:78
  363.7 34.9 %all-reduce.6 = (bf16[4,2048]{1,0:T(4,128)(2,1)S(1)}, bf16[4]{0:T(256)(128)(2,1)S(1)}) all-reduce(bf16[4,2048]{1,0:T(4,128)(2,1)S(1)} %fusion.46, bf16[4]{0:T(256)(128)(2,1)S(1)} %get-tuple-element.276), channel_id=1, replica_groups=mesh['pair'=4,'row'=8] {'row'}, use_global_device_ids=true, to_apply=%region_4.4 | all-reduce | flops 8196 | bytes 32784 | tf_op jit(solution)/shard_map/while/body/eval_jaxpr/pmax | solution.py:69
  399.5 4.8 select_reduce_fusion.13
  404.2 33.3 %all-reduce.7 = (f32[4,2048]{1,0:T(4,128)S(1)}, f32[4]{0:T(128)S(1)}) all-reduce(f32[4,2048]{1,0:T(4,128)S(1)} %select_reduce_fusion.13, f32[4]{0:T(128)S(1)} %select_reduce_fusion.14), channel_id=1, replica_groups=mesh['pair'=4,'row'=8] {'row'}, use_global_device_ids=true, to_apply=%region_8.8 | all-reduce | flops 8196 | bytes 65568 | tf_op jit(solution)/shard_map/while/body/eval_jaxpr/psum | solution.py:78
  450.4 34.9 %all-reduce.6 = (bf16[4,2048]{1,0:T(4,128)(2,1)S(1)}, bf16[4]{0:T(256)(128)(2,1)S(1)}) all-reduce(bf16[4,2048]{1,0:T(4,128)(2,1)S(1)} %fusion.46, bf16[4]{0:T(256)(128)(2,1)S(1)} %get-tuple-element.276), channel_id=1, replica_groups=mesh['pair'=4,'row'=8] {'row'}, use_global_device_ids=true, to_apply=%region_4.4 | all-reduce | flops 8196 | bytes 32784 | tf_op jit(solution)/shard_map/while/body/eval_jaxpr/pmax | solution.py:69
  486.1 4.8 select_reduce_fusion.13
  490.9 33.3 %all-reduce.7 = (f32[4,2048]{1,0:T(4,128)S(1)}, f32[4]{0:T(128)S(1)}) all-reduce(f32[4,2048]{1,0:T(4,128)S(1)} %select_reduce_fusion.13, f32[4]{0:T(128)S(1)} %select_reduce_fusion.14), channel_id=1, replica_groups=mesh['pair'=4,'row'=8] {'row'}, use_global_device_ids=true, to_apply=%region_8.8 | all-reduce | flops 8196 | bytes 65568 | tf_op jit(solution)/shard_map/while/body/eval_jaxpr/psum | solution.py:78
  537.1 35.0 %all-reduce.6 = (bf16[4,2048]{1,0:T(4,128)(2,1)S(1)}, bf16[4]{0:T(256)(128)(2,1)S(1)}) all-reduce(bf16[4,2048]{1,0:T(4,128)(2,1)S(1)} %fusion.46, bf16[4]{0:T(256)(128)(2,1)S(1)} %get-tuple-element.276), channel_id=1, replica_groups=mesh['pair'=4,'row'=8] {'row'}, use_global_device_ids=true, to_apply=%region_4.4 | all-reduce | flops 8196 | bytes 32784 | tf_op jit(solution)/shard_map/while/body/eval_jaxpr/pmax | solution.py:69
  572.9 4.8 select_reduce_fusion.13
  577.7 33.3 %all-reduce.7 = (f32[4,2048]{1,0:T(4,128)S(1)}, f32[4]{0:T(128)S(1)}) all-reduce(f32[4,2048]{1,0:T(4,128)S(1)} %select_reduce_fusion.13, f32[4]{0:T(128)S(1)} %select_reduce_fusion.14), channel_id=1, replica_groups=mesh['pair'=4,'row'=8] {'row'}, use_global_device_ids=true, to_apply=%region_8.8 | all-reduce | flops 8196 | bytes 65568 | tf_op jit(solution)/shard_map/while/body/eval_jaxpr/psum | solution.py:78
  623.8 34.9 %all-reduce.6 = (bf16[4,2048]{1,0:T(4,128)(2,1)S(1)}, bf16[4]{0:T(256)(128)(2,1)S(1)}) all-reduce(bf16[4,2048]{1,0:T(4,128)(2,1)S(1)} %fusion.46, bf16[4]{0:T(256)(128)(2,1)S(1)} %get-tuple-element.276), channel_id=1, replica_groups=mesh['pair'=4,'row'=8] {'row'}, use_global_device_ids=true, to_apply=%region_4.4 | all-reduce | flops 8196 | bytes 32784 | tf_op jit(solution)/shard_map/while/body/eval_jaxpr/pmax | solution.py:69
  659.5 4.8 select_reduce_fusion.13
  664.3 33.3 %all-reduce.7 = (f32[4,2048]{1,0:T(4,128)S(1)}, f32[4]{0:T(128)S(1)}) all-reduce(f32[4,2048]{1,0:T(4,128)S(1)} %select_reduce_fusion.13, f32[4]{0:T(128)S(1)} %select_reduce_fusion.14), channel_id=1, replica_groups=mesh['pair'=4,'row'=8] {'row'}, use_global_device_ids=true, to_apply=%region_8.8 | all-reduce | flops 8196 | bytes 65568 | tf_op jit(solution)/shard_map/while/body/eval_jaxpr/psum | solution.py:78
  710.5 34.9 %all-reduce.6 = (bf16[4,2048]{1,0:T(4,128)(2,1)S(1)}, bf16[4]{0:T(256)(128)(2,1)S(1)}) all-reduce(bf16[4,2048]{1,0:T(4,128)(2,1)S(1)} %fusion.46, bf16[4]{0:T(256)(128)(2,1)S(1)} %get-tuple-element.276), channel_id=1, replica_groups=mesh['pair'=4,'row'=8] {'row'}, use_global_device_ids=true, to_apply=%region_4.4 | all-reduce | flops 8196 | bytes 32784 | tf_op jit(solution)/shard_map/while/body/eval_jaxpr/pmax | solution.py:69
  746.2 4.8 select_reduce_fusion.13
  751.0 33.3 %all-reduce.7 = (f32[4,2048]{1,0:T(4,128)S(1)}, f32[4]{0:T(128)S(1)}) all-reduce(f32[4,2048]{1,0:T(4,128)S(1)} %select_reduce_fusion.13, f32[4]{0:T(128)S(1)} %select_reduce_fusion.14), channel_id=1, replica_groups=mesh['pair'=4,'row'=8] {'row'}, use_global_device_ids=true, to_apply=%region_8.8 | all-reduce | flops 8196 | bytes 65568 | tf_op jit(solution)/shard_map/while/body/eval_jaxpr/psum | solution.py:78
  797.1 34.9 %all-reduce.6 = (bf16[4,2048]{1,0:T(4,128)(2,1)S(1)}, bf16[4]{0:T(256)(128)(2,1)S(1)}) all-reduce(bf16[4,2048]{1,0:T(4,128)(2,1)S(1)} %fusion.46, bf16[4]{0:T(256)(128)(2,1)S(1)} %get-tuple-element.276), channel_id=1, replica_groups=mesh['pair'=4,'row'=8] {'row'}, use_global_device_ids=true, to_apply=%region_4.4 | all-reduce | flops 8196 | bytes 32784 | tf_op jit(solution)/shard_map/while/body/eval_jaxpr/pmax | solution.py:69
  837.7 33.3 %all-reduce.7 = (f32[4,2048]{1,0:T(4,128)S(1)}, f32[4]{0:T(128)S(1)}) all-reduce(f32[4,2048]{1,0:T(4,128)S(1)} %select_reduce_fusion.13, f32[4]{0:T(128)S(1)} %select_reduce_fusion.14), channel_id=1, replica_groups=mesh['pair'=4,'row'=8] {'row'}, use_global_device_ids=true, to_apply=%region_8.8 | all-reduce | flops 8196 | bytes 65568 | tf_op jit(solution)/shard_map/while/body/eval_jaxpr/psum | solution.py:78
  883.8 34.9 %all-reduce.6 = (bf16[4,2048]{1,0:T(4,128)(2,1)S(1)}, bf16[4]{0:T(256)(128)(2,1)S(1)}) all-reduce(bf16[4,2048]{1,0:T(4,128)(2,1)S(1)} %fusion.46, bf16[4]{0:T(256)(128)(2,1)S(1)} %get-tuple-element.276), channel_id=1, replica_groups=mesh['pair'=4,'row'=8] {'row'}, use_global_device_ids=true, to_apply=%region_4.4 | all-reduce | flops 8196 | bytes 32784 | tf_op jit(solution)/shard_map/while/body/eval_jaxpr/pmax | solution.py:69
  924.3 33.3 %all-reduce.7 = (f32[4,2048]{1,0:T(4,128)S(1)}, f32[4]{0:T(128)S(1)}) all-reduce(f32[4,2048]{1,0:T(4,128)S(1)} %select_reduce_fusion.13, f32[4]{0:T(128)S(1)} %select_reduce_fusion.14), channel_id=1, replica_groups=mesh['pair'=4,'row'=8] {'row'}, use_global_device_ids=true, to_apply=%region_8.8 | all-reduce | flops 8196 | bytes 65568 | tf_op jit(solution)/shard_map/while/body/eval_jaxpr/psum | solution.py:78
  962.5 6.5 subtract_select_fusion
  (193 shorter events, 154.0 us)
Async XLA Ops:
  7.2 1.3 copy-start
  7.2 79.1 %all-gather.3.cloned.1.call-start = ((), (), s32[]{:S(2)}) async-start(), calls=%async_computation | async-start | bytes 4718592 | tf_op jit(solution)/shard_map/all_gather | solution.py:40
  93.1 5.8 copy-start.1
  102.6 41.5 %copy-start.2 = (f32[4,256]{1,0:T(4,128)}, f32[4,256]{1,0:T(4,128)S(1)}, u32[]{:S(2)}) copy-start(f32[4,256]{1,0:T(4,128)S(1)} %get-tuple-element.329) | copy-start | bytes 12292 | tf_op jit(solution)/shard_map/while
  179.7 5.8 copy-start.1
  189.1 41.7 %copy-start.2 = (f32[4,256]{1,0:T(4,128)}, f32[4,256]{1,0:T(4,128)S(1)}, u32[]{:S(2)}) copy-start(f32[4,256]{1,0:T(4,128)S(1)} %get-tuple-element.329) | copy-start | bytes 12292 | tf_op jit(solution)/shard_map/while
  266.4 5.8 copy-start.1
  275.8 41.7 %copy-start.2 = (f32[4,256]{1,0:T(4,128)}, f32[4,256]{1,0:T(4,128)S(1)}, u32[]{:S(2)}) copy-start(f32[4,256]{1,0:T(4,128)S(1)} %get-tuple-element.329) | copy-start | bytes 12292 | tf_op jit(solution)/shard_map/while
  353.0 5.8 copy-start.1
  362.5 41.7 %copy-start.2 = (f32[4,256]{1,0:T(4,128)}, f32[4,256]{1,0:T(4,128)S(1)}, u32[]{:S(2)}) copy-start(f32[4,256]{1,0:T(4,128)S(1)} %get-tuple-element.329) | copy-start | bytes 12292 | tf_op jit(solution)/shard_map/while
  439.8 5.8 copy-start.1
  449.2 41.7 %copy-start.2 = (f32[4,256]{1,0:T(4,128)}, f32[4,256]{1,0:T(4,128)S(1)}, u32[]{:S(2)}) copy-start(f32[4,256]{1,0:T(4,128)S(1)} %get-tuple-element.329) | copy-start | bytes 12292 | tf_op jit(solution)/shard_map/while
  526.4 5.8 copy-start.1
  535.9 41.8 %copy-start.2 = (f32[4,256]{1,0:T(4,128)}, f32[4,256]{1,0:T(4,128)S(1)}, u32[]{:S(2)}) copy-start(f32[4,256]{1,0:T(4,128)S(1)} %get-tuple-element.329) | copy-start | bytes 12292 | tf_op jit(solution)/shard_map/while
  613.2 5.8 copy-start.1
  622.6 41.7 %copy-start.2 = (f32[4,256]{1,0:T(4,128)}, f32[4,256]{1,0:T(4,128)S(1)}, u32[]{:S(2)}) copy-start(f32[4,256]{1,0:T(4,128)S(1)} %get-tuple-element.329) | copy-start | bytes 12292 | tf_op jit(solution)/shard_map/while
  699.8 5.8 copy-start.1
  709.3 41.7 %copy-start.2 = (f32[4,256]{1,0:T(4,128)}, f32[4,256]{1,0:T(4,128)S(1)}, u32[]{:S(2)}) copy-start(f32[4,256]{1,0:T(4,128)S(1)} %get-tuple-element.329) | copy-start | bytes 12292 | tf_op jit(solution)/shard_map/while
  786.5 5.8 copy-start.1
  796.0 41.7 %copy-start.2 = (f32[4,256]{1,0:T(4,128)}, f32[4,256]{1,0:T(4,128)S(1)}, u32[]{:S(2)}) copy-start(f32[4,256]{1,0:T(4,128)S(1)} %get-tuple-element.329) | copy-start | bytes 12292 | tf_op jit(solution)/shard_map/while
  873.2 5.8 copy-start.1
  882.6 41.7 %copy-start.2 = (f32[4,256]{1,0:T(4,128)}, f32[4,256]{1,0:T(4,128)S(1)}, u32[]{:S(2)}) copy-start(f32[4,256]{1,0:T(4,128)S(1)} %get-tuple-element.329) | copy-start | bytes 12292 | tf_op jit(solution)/shard_map/while
Sparse Core Ops, SparseCore 0:
  10.7 75.4 all-gather.2
where the time goes:
time: 977 us; the launch traced here: 976 us
  blocking collectives  682 us (70%)
  other arithmetic  192 us (20%)
  waiting for transfers between devices  72.5 us (7%)
  between operations  14.8 us (2%)
    pmax x10, blocking collectives, column_pass(): lax.pmax(jnp.max(shifted, axis=1).astype(jnp.bfloat16), 'row')  349 us
    psum x10, blocking collectives, column_pass(): totals, bin_total = lax.psum((totals, bin_total), 'row')  333 us
    all_gather x1, waiting for transfers between devices, on_device(): lax.all_gather(col_desc, 'row', axis=1, tiled=True)  72.5 us
    reduce_max x20, other arithmetic, local_stats(): peaks = jnp.max(shifted, axis=reduce_dim)  55.3 us
    reduce_sum x10, other arithmetic, column_pass(): jnp.sum(jnp.where(row_kept[:, :, None], jnp.exp(shifted - peaks[:, None,...  47.7 us
    reduce_sum x20, other arithmetic, local_stats(): jnp.sum(jnp.where(kept, jnp.exp(shifted - jnp.expand_dims(peaks, reduce_d...  30.3 us
  transfers between devices with their start and end apart: 1, of which 1 were waited for; matrix products, arithmetic and copies ran while one was open for 0% of the time, Pallas kernels for 0%

commit v1 on v0

v1 whole, which is shorter than its diff:
```python
import functools

import jax
import jax.numpy as jnp
from jax import lax
from jax.experimental import pallas as pl
from jax.experimental.pallas import tpu as pltpu
from jax.sharding import PartitionSpec as P

ITERS = 10
LIFT = 40.0
LANES = 128
BLOCK = 128
MESH = pl.DeviceIdType.MESH
NT = (((1,), (1,)), ((), ()))


def sinkhorn_kernel(
    teams, size, counts, pairs, bin_score, desc, imgs, fin,
    rowsel, colsel, rows, own, kern, peak, kbin, mass, left, b8, bbin, abin, xbuf, fin_send,
    crit_send, crit_recv, fwd_send, fwd_recv, bulk_send, bulk_recv, ex_send, ex_recv, fin_ssem, fin_rsem, local_sem,
):
    me = lax.axis_index("row")
    team, member = me // size, me % size
    local, depth = rows.shape[1], rows.shape[2]
    height, cols = kern.shape
    blocks = height // BLOCK

    def device(t, m):
        return {"row": t * size + m}

    def remote(src, dst, ssem, rsem, t, m):
        return pltpu.make_async_remote_copy(
            src_ref=src, dst_ref=dst, send_sem=ssem, recv_sem=rsem, device_id=device(t, m), device_id_type=MESH
        )

    barrier = pltpu.get_barrier_semaphore()
    for dz in range(1, teams):
        pl.semaphore_signal(barrier, inc=1, device_id=device((team + dz) % teams, member), device_id_type=MESH)
    for d in range(1, size):
        pl.semaphore_signal(barrier, inc=1, device_id=device(team, (member + d) % size), device_id_type=MESH)

    for p in range(teams):
        colsel[p] = desc[pairs[p, 1]]
        rowsel[p] = desc[pairs[p, 0]]
    own[team, member] = colsel[team]
    rows[team] = rowsel[team]
    pl.semaphore_wait(barrier, teams + size - 2)

    crit = {}
    for dz in range(1, teams):
        to = (team + dz) % teams
        crit[0, dz] = remote(colsel.at[to], own.at[team, member], crit_send.at[0, dz], crit_recv.at[0, dz], to, member)
        crit[0, dz].start()
    for dz in range(1, teams):
        to = (team + dz) % teams
        crit[1, dz] = remote(rowsel.at[to], rows.at[team], crit_send.at[1, dz], crit_recv.at[1, dz], to, member)
        crit[1, dz].start()
    fwd = {}
    for dz in range(teams):
        if dz:
            crit[0, dz].wait_recv()
        source = (team + teams - dz) % teams
        for d in range(1, size):
            fwd[dz, d] = remote(
                own.at[source, member], own.at[source, member], fwd_send.at[dz, d], fwd_recv.at[dz, d],
                team, (member + d) % size,
            )
            fwd[dz, d].start()

    hops = (teams - 1) // 2
    split = teams % 2 == 0
    half = (size + 1) // 2

    def bulk(way, hop, d):
        step = 1 if way == 0 else teams - 1
        to = (team + step) % teams
        image = (team + (teams - step) * hop) % teams
        part = (member + d) % size
        src = own.at[:, part] if hop == 0 else imgs.at[image, :, part]
        return remote(src, imgs.at[image, :, part], bulk_send.at[way, hop, d], bulk_recv.at[way, hop, d], to, member)

    def carried(way, hop):
        if hop < hops:
            return list(range(size))
        if hop == hops and split:
            return list(range(half)) if way == 0 else list(range(half, size))
        return []

    for way in (0, 1):
        if 0 in carried(way, 0):
            bulk(way, 0, 0).start()
    for dz in range(teams):
        for d in range(1, size):
            fwd[dz, d].wait_recv()
    for d in range(1, size):
        for way in (0, 1):
            if d in carried(way, 0):
                bulk(way, 0, d).start()
    keep = pltpu.make_async_copy(own, imgs.at[team], local_sem)
    keep.start()
    for dz in range(1, teams):
        crit[1, dz].wait_recv()

    na_i, nb_i = counts[pairs[team, 0]], counts[pairs[team, 1]]
    line = jnp.ones((1, LANES), jnp.float32)
    na, nb = line * na_i.astype(jnp.float32), line * nb_i.astype(jnp.float32)
    norm = 1.0 / (na + nb)
    mu_bin, nu_bin = nb * norm, na * norm
    bin_value = bin_score[0]
    wide = lax.broadcasted_iota(jnp.int32, (8, cols), 1) < nb_i

    chunk = 512 if cols % 512 == 0 else LANES * size
    per = chunk // local
    flat = own.reshape(teams * size * local, depth)

    @pl.loop(0, teams)
    def _(s):
        block = rows[s]

        @pl.loop(0, cols // chunk)
        def _(n):
            at = pl.multiple_of(n * chunk, chunk)
            part = lax.dot_general(block, flat[pl.ds(at, chunk), :], NT, preferred_element_type=jnp.float32)
            kern[pl.ds(pl.multiple_of(s * local, local), local), pl.ds(at, chunk)] = part * (depth ** -0.5)

    def tree(terms, op):
        while len(terms) > 1:
            terms = [op(terms[i], terms[i + 1]) if i + 1 < len(terms) else terms[i] for i in range(0, len(terms), 2)]
        return terms[0]

    def lanes(x):
        return [x[:, i * LANES : (i + 1) * LANES] for i in range(cols // LANES)]

    @pl.loop(0, height // 64)
    def _(g):
        for i in range(8):
            at = pl.multiple_of(g * 64 + i * 8, 8)
            x = jnp.where(wide, kern[pl.ds(at, 8), :], -1e30)
            top = jnp.max(tree(lanes(x), jnp.maximum), axis=1, keepdims=True)
            top = jnp.maximum(top, bin_value) - LIFT
            kern[pl.ds(at, 8), :] = jnp.exp(x - top)
            peak[pl.ds(at, 8), :] = top
            kbin[pl.ds(at, 8), :] = jnp.exp(bin_value - top)
            slot = at // local
            index = (slot * size + member) * local + at % local + lax.broadcasted_iota(jnp.int32, (8, 1), 0)
            mass[pl.ds(at, 8), :] = jnp.where(index < na_i, norm[:, :1], 0.0)

    b8[...] = jnp.where(wide, 1.0, 0.0)
    bbin[...] = jnp.ones_like(bbin)

    def row_part(g):
        for i in range(BLOCK // 8):
            at = pl.multiple_of(g * BLOCK + i * 8, 8)
            total = jnp.sum(tree(lanes(kern[pl.ds(at, 8), :] * b8[...]), jnp.add), axis=1, keepdims=True)
            total = total + kbin[pl.ds(at, 8), :] * bbin[:, :1]
            left[pl.ds(at, 8), :] = mass[pl.ds(at, 8), :] / total

    def col_part(g, sums):
        acc, edge = sums
        for i in range(BLOCK // 8):
            at = pl.multiple_of(g * BLOCK + i * 8, 8)
            a = left[pl.ds(at, 8), :]
            acc = acc + kern[pl.ds(at, 8), :] * a
            edge = edge + kbin[pl.ds(at, 8), :] * a
        return acc, edge

    def exchange(slot, d):
        return remote(
            xbuf.at[slot, member], xbuf.at[slot, member], ex_send.at[slot, d], ex_recv.at[slot, d],
            team, (member + d) % size,
        )

    def sweep(it, _):
        slot = it % 2
        row_part(0)

        def step(g, sums):
            sums = col_part(g - 1, sums)
            row_part(g)
            return sums

        sums = (jnp.zeros((8, cols), jnp.float32), jnp.zeros((8, 1), jnp.float32))
        sums = lax.fori_loop(1, blocks, step, sums)
        acc, edge = col_part(blocks - 1, sums)
        xbuf[slot, member, :, :cols] = jnp.sum(acc, axis=0, keepdims=True)
        xbuf[slot, member, :, cols:] = jnp.broadcast_to(jnp.sum(edge, axis=0, keepdims=True), (1, LANES))
        for d in range(1, size):
            exchange(slot, d).start()
        all_b = jnp.sum(tree(lanes(b8[0:1, :]), jnp.add), axis=1, keepdims=True) + bbin[0:1, :1]
        row_bin = mu_bin / all_b
        abin[...] = row_bin
        for hop in range(1, teams):
            for way in (0, 1):
                for d in carried(way, hop):
                    @pl.when(it == min(ITERS - 1, 4 * hop + d))
                    def _():
                        bulk(way, hop - 1, d).wait_recv()
                        bulk(way, hop, d).start()
        for d in range(1, size):
            exchange(slot, d).wait()
        total = xbuf[slot, 0]
        for k in range(1, size):
            total = total + xbuf[slot, k]
        total = total + row_bin[:, :1]
        fresh = norm[:, :1] / total[:, :cols]
        fin_send[0, :, :cols] = fresh
        b8[...] = jnp.where(wide, fresh, 0.0)
        bbin[...] = jnp.broadcast_to(nu_bin / total[:, cols:], bbin.shape)
        return 0

    lax.fori_loop(0, ITERS, sweep, 0)

    col_pot = jnp.log(fin_send[0, :, :cols])
    col_bin = jnp.log(bbin[0:1, :])
    row_bin = jnp.log(abin[...]) - bin_value
    eye = lax.broadcasted_iota(jnp.int32, (LANES, LANES), 0) == lax.broadcasted_iota(jnp.int32, (LANES, LANES), 1)
    for t in range(teams):
        fin_send[t, :, :cols] = col_pot
        fin_send[t, :, cols : cols + LANES] = col_bin
        fin_send[t, :, cols + LANES : cols + 2 * LANES] = row_bin
        for i in range(local // LANES):
            at = pl.ds(t * local + i * LANES, LANES)
            pot = jnp.log(jnp.maximum(left[at, :], 1e-37)) - peak[at, :]
            flat_pot = jnp.sum(jnp.where(eye, pot, 0.0), axis=0, keepdims=True)
            fin_send[t, :, cols + (2 + i) * LANES : cols + (3 + i) * LANES] = flat_pot
    sent = []
    for dz in range(1, teams):
        to = (team + dz) % teams
        sent.append(remote(fin_send.at[to], fin.at[team], fin_ssem.at[dz], fin_rsem.at[dz], to, member))
        sent[-1].start()
    fin[team] = fin_send[team]

    for dz in range(1, teams):
        crit[0, dz].wait_send()
        crit[1, dz].wait_send()
    for dz in range(teams):
        for d in range(1, size):
            fwd[dz, d].wait_send()
    keep.wait()
    for hop in range(teams):
        for way in (0, 1):
            for d in carried(way, hop):
                bulk(way, hop, d).wait_send()
                if d not in carried(way, hop + 1):
                    bulk(way, hop, d).wait_recv()
    for copy in sent:
        copy.wait()


def finish_kernel(size, counts, pairs, bin_score, rowdesc, image, fin, log_match, row_bins, col_bins):
    p = pl.program_id(0)
    me = lax.axis_index("row")
    local, depth = rowdesc.shape[1:]
    cols = log_match.shape[2]
    na_i, nb_i = counts[pairs[p, 0]], counts[pairs[p, 1]]
    line = jnp.ones((1, LANES), jnp.float32)
    log_norm = -jnp.log(line * (na_i + nb_i).astype(jnp.float32))[:, :1]
    bin_value = bin_score[0]
    col_pot = fin[0, :, :cols]
    col_bin = fin[0, :, cols : cols + 1]
    row_bin = fin[0, :, cols + LANES : cols + LANES + 1]
    flat_pot = fin[0, :, cols + 2 * LANES :]
    wide = lax.broadcasted_iota(jnp.int32, (1, cols), 1) < nb_i
    row_index = me * local + lax.broadcasted_iota(jnp.int32, (1, local), 1)
    row_bins[pl.ds(p, 1), :] = jnp.where(row_index < na_i, bin_value + flat_pot + col_bin - log_norm, 0.0)
    col_bins[pl.ds(p, 1), :] = jnp.where(wide, bin_value + row_bin + col_pot - log_norm, 0.0)
    eye = lax.broadcasted_iota(jnp.int32, (LANES, LANES), 0) == lax.broadcasted_iota(jnp.int32, (LANES, LANES), 1)
    tops = []
    for i in range(local // LANES):
        piece = flat_pot[:, i * LANES : (i + 1) * LANES]
        tops.append(jnp.sum(jnp.where(eye, piece, 0.0), axis=1, keepdims=True))
    row_pot = jnp.concatenate(tops, axis=0)
    tall = me * local + lax.broadcasted_iota(jnp.int32, (local, 1), 0) < na_i
    flat = image.reshape(cols, depth)
    chunk = 512 if cols % 512 == 0 else LANES
    block = rowdesc[0]
    for n in range(cols // chunk):
        at = slice(n * chunk, (n + 1) * chunk)
        scores = lax.dot_general(block, flat[at, :], NT, preferred_element_type=jnp.float32) * (depth ** -0.5)
        value = scores + row_pot + col_pot[:, at] - log_norm
        log_match[0, :, at] = jnp.where(tall & wide[:, at], value, 0.0)


def on_device(teams, size, descriptors, counts, pairs, bin_score):
    images, local, depth = descriptors.shape
    cols = local * teams * size
    height = local * teams
    width = cols + 2 * LANES + local
    vmem = pl.BlockSpec(memory_space=pltpu.VMEM)
    smem = pl.BlockSpec(memory_space=pltpu.SMEM)
    f32, bf16 = jnp.float32, jnp.bfloat16
    dma = pltpu.SemaphoreType.DMA
    imgs, fin = pl.pallas_call(
        functools.partial(sinkhorn_kernel, teams, size),
        out_shape=(
            jax.ShapeDtypeStruct((teams, teams, size, local, depth), bf16),
            jax.ShapeDtypeStruct((teams, 1, width), f32),
        ),
        in_specs=[smem, smem, smem, vmem],
        out_specs=(pl.BlockSpec(memory_space=pl.ANY), vmem),
        scratch_shapes=[
            pltpu.VMEM((teams, local, depth), bf16),
            pltpu.VMEM((teams, local, depth), bf16),
            pltpu.VMEM((teams, local, depth), bf16),
            pltpu.VMEM((teams, size, local, depth), bf16),
            pltpu.VMEM((height, cols), f32),
            pltpu.VMEM((height, 1), f32),
            pltpu.VMEM((height, 1), f32),
            pltpu.VMEM((height, 1), f32),
            pltpu.VMEM((height, 1), f32),
            pltpu.VMEM((8, cols), f32),
            pltpu.VMEM((8, LANES), f32),
            pltpu.VMEM((1, LANES), f32),
            pltpu.VMEM((2, size, 1, cols + LANES), f32),
            pltpu.VMEM((teams, 1, width), f32),
            dma((2, teams)),
            dma((2, teams)),
            dma((teams, size)),
            dma((teams, size)),
            dma((2, teams, size)),
            dma((2, teams, size)),
            dma((2, size)),
            dma((2, size)),
            dma((teams,)),
            dma((teams,)),
            dma,
        ],
        compiler_params=pltpu.CompilerParams(
            collective_id=0, has_side_effects=True, vmem_limit_bytes=48 * 1024 * 1024
        ),
    )(counts, pairs, bin_score, descriptors)
    return pl.pallas_call(
        functools.partial(finish_kernel, size),
        out_shape=(
            jax.ShapeDtypeStruct((teams, local, cols), f32),
            jax.ShapeDtypeStruct((teams, local), f32),
            jax.ShapeDtypeStruct((teams, cols), f32),
        ),
        grid_spec=pltpu.PrefetchScalarGridSpec(
            num_scalar_prefetch=3,
            grid=(teams,),
            in_specs=[
                pl.BlockSpec((1, local, depth), lambda p, c, q, b: (q[p, 0], 0, 0)),
                pl.BlockSpec((1, teams, size, local, depth), lambda p, c, q, b: (p, 0, 0, 0, 0)),
                pl.BlockSpec((1, 1, width), lambda p, c, q, b: (p, 0, 0)),
            ],
            out_specs=(
                pl.BlockSpec((1, local, cols), lambda p, c, q, b: (p, 0, 0)),
                pl.BlockSpec((teams, local), lambda p, c, q, b: (0, 0)),
                pl.BlockSpec((teams, cols), lambda p, c, q, b: (0, 0)),
            ),
        ),
    )(counts, pairs, bin_score, descriptors, imgs, fin)


def solution(mesh):
    group = mesh.shape["row"]

    def body(descriptors, counts, pairs, bin_score):
        teams = pairs.shape[0]
        return on_device(teams, group // teams, descriptors, counts, pairs, bin_score)

    return jax.shard_map(
        body,
        mesh=mesh,
        in_specs=(P("pair", "row", None), P("pair"), P("pair", None), P()),
        out_specs=(P("pair", "row", None), P("pair", "row"), P("pair", None)),
        check_vma=False,
    )
```

time: 977 us -> 122 us (0.12)
  blocking collectives: 682 us -> 0 us
  other arithmetic: 192 us -> 0 us
  Pallas kernels: 0 us -> 115 us
  waiting for transfers between devices: 72.5 us -> 0 us
  between operations: 14.8 us -> 1.3 us
    pmax x10 -> x0, blocking collectives: 349 us -> none  [column_pass(): lax.pmax(jnp.max(shifted, axis=1).astype(jnp.bfloat16), 'row')]
    psum x10 -> x0, blocking collectives: 333 us -> none  [column_pass(): totals, bin_total = lax.psum((totals, bin_total), 'row')]
    pallas_call x0 -> x2, Pallas kernels: none -> 115 us  [the longest x1 107 us: on_device(): pl.pallas_call(functools.partial(sinkhorn_kernel, teams, size), out_shape...]
    reduce_sum x40 -> x0, other arithmetic: 86.3 us -> none  [the longest x10 47.7 us: column_pass(): jnp.sum(jnp.where(row_kept[:, :, None], jnp.exp(shifted - peaks[:, None,...]
    reduce_max x40 -> x0, other arithmetic: 75.3 us -> none  [the longest x20 55.3 us: local_stats(): peaks = jnp.max(shifted, axis=reduce_dim)]
    all_gather x1 -> x0, waiting for transfers between devices: 72.5 us -> none  [on_device(): lax.all_gather(col_desc, 'row', axis=1, tiled=True)]
    sub x20 -> x0, other arithmetic: 12.9 us -> none  [the longest x10 11.8 us: column_pass(): col_bin = nu_bin - finish(bin_peak, bin_total, bin_extra)]
  transfers between devices with their start and end apart: 1 -> 0, of which waited for: 1 -> 0; matrix products, arithmetic and copies ran while one was open for 0% -> 0% of each run, Pallas kernels for 0% -> 0%
where the time goes in v1:
time: 122 us
  Pallas kernels  115 us (94%)
  local copies, waits for them, and re-layouts  5.19 us (4%)
  between operations  1.3 us (1%)
    pallas_call x1, Pallas kernels, on_device(): pl.pallas_call(functools.partial(sinkhorn_kernel, teams, size), out_shape...  107 us
    pallas_call x1, Pallas kernels, on_device(): pl.pallas_call(functools.partial(finish_kernel, size), out_shape=(jax.Sha...  7.84 us
    unnamed x11, local copies, waits for them, and re-layouts  5.19 us

profile of v1, /device:TPU:0, one launch (start us, length us, event | category | flops | bytes accessed | tf_op | source)
XLA Modules:
  0.0 121.8 jit_solution(1357627878794785965)
XLA Ops:
  1.3 0.8 copy.8.pairs
  2.0 0.0 copy-start.1
  2.0 1.2 %copy-done.1 = bf16[8,256,256]{2,1,0:T(8,128)(2,1)S(1)} copy-done((bf16[8,256,256]{2,1,0:T(8,128)(2,1)S(1)}, bf16[8,256,256]{2,1,0:T(8,128)(2,1)}, u32[]{:S(2)}) %copy-start.1) | copy-done | bytes 1048600
  3.3 0.0 copy-start.4
  3.3 0.7 copy-done.4
  3.9 0.0 copy-start.3
  3.9 107.4 %shard_map.67 = (bf16[4,4,2,256,256]{4,3,2,1,0:T(8,128)(2,1)S(1)}, f32[4,1,2560]{2,1,0:T(1,128)S(1)}) custom-call(s32[8]{0:T(128)S(1)} %copy-done.4, s32[4,2]{1,0:T(4,128)S(1)} %copy.8.pairs, f32[1]{0:T(128)S(6)} %copy.9.bin_score, bf16[8,256,256]{2,1,0:T(8,128)(2,1)S(1)} %copy-done.1), custom_call_target="tpu_custom_call" | custom-call | tf_op jit(solution)/shard_map/pallas_call | solution.py:294
  111.4 0.0 copy-start
  111.4 1.9 %copy-done = bf16[4,4,2,256,256]{4,3,2,1,0:T(8,128)(2,1)} copy-done((bf16[4,4,2,256,256]{4,3,2,1,0:T(8,128)(2,1)}, bf16[4,4,2,256,256]{4,3,2,1,0:T(8,128)(2,1)S(1)}, u32[]{:S(2)}) %copy-start) | copy-done | bytes 4194328
  113.3 0.0 copy-start.2
  113.3 0.6 copy-done.2
  113.9 0.0 copy-done.3
  113.9 7.8 %shard_map.68 = (f32[4,256,2048]{2,1,0:T(8,128)}, f32[4,256]{1,0:T(4,128)}, f32[4,2048]{1,0:T(4,128)}) custom-call(s32[8]{0:T(128)} %counts.3, s32[4,2]{1,0:T(4,128)} %copy-done.3, f32[1]{0:T(128)S(6)} %copy.9.bin_score, bf16[8,256,256]{2,1,0:T(8,128)(2,1)} %rowdesc.1, bf16[4,4,2,256,256]{4,3,2,1,0:T(8,128)(2,1)} %copy-done, f32[4,1,2560]{2,1,0:T(1,128)} %copy-done.2), custom_call_target="tpu_custom_call" | custom-call | tf_op jit(solution)/shard_map/pallas_call | solution.py:333
Async XLA Ops:
  2.0 1.2 %copy-start.1 = (bf16[8,256,256]{2,1,0:T(8,128)(2,1)S(1)}, bf16[8,256,256]{2,1,0:T(8,128)(2,1)}, u32[]{:S(2)}) copy-start(bf16[8,256,256]{2,1,0:T(8,128)(2,1)} %rowdesc.1) | copy-start | bytes 3145732
  3.3 0.7 copy-start.4
  3.9 110.0 %copy-start.3 = (s32[4,2]{1,0:T(4,128)}, s32[4,2]{1,0:T(4,128)S(1)}, u32[]{:S(2)}) copy-start(s32[4,2]{1,0:T(4,128)S(1)} %copy.8.pairs) | copy-start | bytes 100
  111.4 1.9 %copy-start = (bf16[4,4,2,256,256]{4,3,2,1,0:T(8,128)(2,1)}, bf16[4,4,2,256,256]{4,3,2,1,0:T(8,128)(2,1)S(1)}, u32[]{:S(2)}) copy-start(bf16[4,4,2,256,256]{4,3,2,1,0:T(8,128)(2,1)S(1)} %get-tuple-element.5.image) | copy-start | bytes 12582916
  113.3 0.6 copy-start.2

commit v2 on v1

v2 whole, which is shorter than its diff:
```python
import functools

import jax
import jax.numpy as jnp
from jax import lax
from jax.experimental import pallas as pl
from jax.experimental.pallas import tpu as pltpu
from jax.sharding import PartitionSpec as P

ITERS = 10
LIFT = 40.0
LANES = 128
BLOCK = 128
MESH = pl.DeviceIdType.MESH
NT = (((1,), (1,)), ((), ()))


def sinkhorn_kernel(
    teams, size, counts, pairs, bin_score, desc, imgs, fin,
    rowsel, colsel, rows, own, score, kern, peak, kbin, mass, left, part, b8, bbin, abin, fin_send,
    crit_send, crit_recv, fwd_send, fwd_recv, bulk_send, bulk_recv, side_send, side_recv, fin_ssem, fin_rsem, local_sem,
):
    me = lax.axis_index("row")
    team, member = me // size, me % size
    local, depth = rows.shape[2:]
    height, cols = kern.shape
    blocks = height // BLOCK

    def device(t, m):
        return {"row": t * size + m}

    def remote(src, dst, ssem, rsem, t, m):
        return pltpu.make_async_remote_copy(
            src_ref=src, dst_ref=dst, send_sem=ssem, recv_sem=rsem, device_id=device(t, m), device_id_type=MESH
        )

    barrier = pltpu.get_barrier_semaphore()
    for dz in range(1, teams):
        pl.semaphore_signal(barrier, inc=1, device_id=device((team + dz) % teams, member), device_id_type=MESH)
    for d in range(1, size):
        pl.semaphore_signal(barrier, inc=1, device_id=device(team, (member + d) % size), device_id_type=MESH)

    for p in range(teams):
        colsel[p] = desc[pairs[p, 1]]
        rowsel[p] = desc[pairs[p, 0]]
    own[team, member] = colsel[team]
    rows[team, member] = rowsel[team]
    pl.semaphore_wait(barrier, teams + size - 2)

    def near(k, sign):
        pick = 0
        for t in range(teams):
            ranked = sorted((o for o in range(teams) if o != t), key=lambda o: (abs(o - t), o))
            pick = pick + jnp.where(team == t, sign * (ranked[k] - t) % teams, 0)
        return pick

    held = ((colsel, own), (rowsel, rows))
    ranks = range(teams - 1)

    def crit(kind, dz):
        to = (team + dz) % teams
        src, dst = held[kind]
        return remote(src.at[to], dst.at[team, member], crit_send.at[kind, dz], crit_recv.at[kind, dz], to, member)

    def fwd(kind, dz, d):
        slot = held[kind][1].at[(team + teams - dz) % teams, member]
        return remote(slot, slot, fwd_send.at[kind, dz, d], fwd_recv.at[kind, dz, d], team, (member + d) % size)

    def hand_over(kind, dz):
        for d in range(1, size):
            fwd(kind, dz, d).start()

    for kind in (0, 1):
        for k in reversed(ranks):
            crit(kind, near(k, 1)).start()
        hand_over(kind, 0)

    def bulk(dz, e):
        to = (team + dz) % teams
        image = (to + e) % teams
        return remote(colsel.at[image], imgs.at[image, team, member], bulk_send.at[dz, e], bulk_recv.at[dz, e], to, member)

    def side(dz, e, d):
        source, image = (team + teams - dz) % teams, (team + e) % teams
        slot = imgs.at[image, source, member]
        src = slot if dz else colsel.at[image]
        return remote(src, slot, side_send.at[dz, e, d], side_recv.at[dz, e, d], team, (member + d) % size)

    def pass_on(dz, e):
        for d in range(1, size):
            side(dz, e, d).start()

    order = [(dz, e) for e in range(1, teams) for dz in range(1, teams)]
    for dz, e in order:
        bulk(dz, e).start()
    keeps = []
    for e in range(1, teams):
        image = (team + e) % teams
        keeps.append(pltpu.make_async_copy(colsel.at[image], imgs.at[image, team, member], local_sem.at[e]))
        keeps[-1].start()
    for k in ranks:
        dz = near(k, -1)
        crit(0, dz).wait_recv()
        hand_over(0, dz)

    na_i, nb_i = counts[pairs[team, 0]], counts[pairs[team, 1]]
    line = jnp.ones((1, LANES), jnp.float32)
    na, nb = line * na_i.astype(jnp.float32), line * nb_i.astype(jnp.float32)
    norm = 1.0 / (na + nb)
    mu_bin, nu_bin = nb * norm, na * norm
    bin_value = bin_score[0]
    wide = lax.broadcasted_iota(jnp.int32, (8, cols), 1) < nb_i
    chunk = 512 if cols % 512 == 0 else LANES
    flat = own.reshape(cols, depth)
    spans = range(cols // LANES)

    def tree(terms, op):
        while len(terms) > 1:
            terms = [op(terms[i], terms[i + 1]) if i + 1 < len(terms) else terms[i] for i in range(0, len(terms), 2)]
        return terms[0]

    def lanes(x):
        return [x[:, i * LANES : (i + 1) * LANES] for i in spans]

    def prepare(source, m):
        s = source * size + m
        block = rows[source, m]

        @pl.loop(0, cols // chunk)
        def _(n):
            at = pl.multiple_of(n * chunk, chunk)
            piece = lax.dot_general(block, flat[pl.ds(at, chunk), :], NT, preferred_element_type=jnp.float32)
            score[:, pl.ds(at, chunk)] = piece * (depth ** -0.5)

        @pl.loop(0, local // 64)
        def _(g):
            tops = []
            for i in range(8):
                x = jnp.where(wide, score[pl.ds(pl.multiple_of(g * 64 + i * 8, 8), 8), :], -1e30)
                top = jnp.max(tree(lanes(x), jnp.maximum), axis=1, keepdims=True)
                tops.append(jnp.maximum(top, bin_value) - LIFT)
            for i, top in enumerate(tops):
                x = score[pl.ds(pl.multiple_of(g * 64 + i * 8, 8), 8), :]
                at = pl.multiple_of(s * local + g * 64 + i * 8, 8)
                kern[pl.ds(at, 8), :] = jnp.where(wide, jnp.exp(x - top), 0.0)
                full = jnp.broadcast_to(top, (8, LANES))
                peak[pl.ds(at, 8), :] = full
                kbin[pl.ds(at, 8), :] = jnp.exp(bin_value - full)
                index = at + lax.broadcasted_iota(jnp.int32, (8, LANES), 0)
                mass[pl.ds(at, 8), :] = jnp.where(index < na_i, norm, 0.0)

    for dz in range(teams):
        for d in range(1, size):
            fwd(0, dz, d).wait_recv()
    keeps.append(pltpu.make_async_copy(own, imgs.at[team], local_sem.at[0]))
    keeps[-1].start()

    def prepare_fwd(dz):
        for d in range(1, size):
            fwd(1, dz, d).wait_recv()
        for d in range(1, size):
            prepare((team + teams - dz) % teams, (member + size - d) % size)

    prepare(team, member)
    behind = 0
    for k in ranks:
        dz = near(k, -1)
        crit(1, dz).wait_recv()
        hand_over(1, dz)
        prepare_fwd(behind)
        prepare((team + teams - dz) % teams, member)
        behind = dz
    prepare_fwd(behind)
    for e in range(1, teams):
        pass_on(0, e)

    b8[...] = jnp.where(wide, 1.0, 0.0)
    bbin[...] = jnp.ones_like(bbin)
    groups = BLOCK // 8

    def row_part(g):
        ats = [pl.ds(pl.multiple_of(g * BLOCK + i * 8, 8), 8) for i in range(groups)]
        accs = [None] * groups
        for c in spans:
            span = slice(c * LANES, (c + 1) * LANES)
            weight = b8[:, span]
            for i, at in enumerate(ats):
                term = kern[at, span] * weight
                accs[i] = term if c == 0 else accs[i] + term
        for i, at in enumerate(ats):
            part[at, :] = accs[i]

    def row_close(g):
        edge = bbin[...]
        ats = [pl.ds(pl.multiple_of(g * BLOCK + i * 8, 8), 8) for i in range(groups)]
        totals = [jnp.broadcast_to(jnp.sum(part[at, :], axis=1, keepdims=True), (8, LANES)) + kbin[at, :] * edge for at in ats]
        for at, total in zip(ats, totals):
            left[at, :] = mass[at, :] / total

    def col_part(g, sums):
        sums = list(sums)
        for i in range(groups):
            at = pl.ds(pl.multiple_of(g * BLOCK + i * 8, 8), 8)
            a = left[at, :]
            for c in spans:
                sums[c] = sums[c] + kern[at, c * LANES : (c + 1) * LANES] * a
            sums[-1] = sums[-1] + kbin[at, :] * a
        return tuple(sums)

    def sweep(it, _):
        row_part(0)
        row_close(0)
        row_part(1)

        def step(g, sums):
            sums = col_part(g - 2, sums)
            row_close(g - 1)
            row_part(g)
            return sums

        zero = jnp.zeros((8, LANES), jnp.float32)
        sums = tuple(zero for _ in spans) + (zero,)
        sums = col_part(blocks - 2, lax.fori_loop(2, blocks, step, sums))
        row_close(blocks - 1)
        sums = col_part(blocks - 1, sums)
        all_b = jnp.sum(tree(lanes(b8[0:1, :]), jnp.add), axis=1, keepdims=True) + bbin[0:1, :1]
        row_bin = mu_bin / all_b
        abin[...] = row_bin
        for c in spans:
            span = slice(c * LANES, (c + 1) * LANES)
            fresh = norm / (jnp.sum(sums[c], axis=0, keepdims=True) + row_bin)
            fin_send[0, :, span] = fresh
            b8[:, span] = jnp.where(wide[:, span], fresh, 0.0)
        edge = jnp.sum(sums[-1], axis=0, keepdims=True) + row_bin
        bbin[...] = jnp.broadcast_to(nu_bin / edge, bbin.shape)
        for k, (dz, e) in enumerate(order):
            @pl.when(it == min(ITERS - 1, k * ITERS // len(order)))
            def _():
                bulk(dz, e).wait_recv()
                pass_on(dz, e)
        return 0

    lax.fori_loop(0, ITERS, sweep, 0)

    col_pot = jnp.log(fin_send[0, :, :cols])
    col_bin = jnp.log(bbin[0:1, :])
    row_bin = jnp.log(abin[...]) - bin_value
    eye = lax.broadcasted_iota(jnp.int32, (LANES, LANES), 0) == lax.broadcasted_iota(jnp.int32, (LANES, LANES), 1)
    for t in range(teams):
        fin_send[t, :, :cols] = col_pot
        fin_send[t, :, cols : cols + LANES] = col_bin
        fin_send[t, :, cols + LANES : cols + 2 * LANES] = row_bin
        for i in range(local // LANES):
            at = pl.ds(pl.multiple_of((t * size + member) * local + i * LANES, LANES), LANES)
            pot = jnp.log(jnp.maximum(left[at, :], 1e-37)) - peak[at, :]
            flat_pot = jnp.sum(jnp.where(eye, pot, 0.0), axis=0, keepdims=True)
            fin_send[t, :, cols + (2 + i) * LANES : cols + (3 + i) * LANES] = flat_pot
    sent = []
    for dz in range(1, teams):
        to = (team + dz) % teams
        sent.append(remote(fin_send.at[to], fin.at[team], fin_ssem.at[dz], fin_rsem.at[dz], to, member))
        sent[-1].start()
    fin[team] = fin_send[team]

    for kind in (0, 1):
        for dz in range(teams):
            if dz:
                crit(kind, dz).wait_send()
            for d in range(1, size):
                fwd(kind, dz, d).wait_send()
    for keep in keeps:
        keep.wait()
    for dz, e in order:
        bulk(dz, e).wait_send()
    for dz in range(teams):
        for e in range(1, teams):
            for d in range(1, size):
                side(dz, e, d).wait()
    for copy in sent:
        copy.wait()


def finish_kernel(size, counts, pairs, bin_score, rowdesc, image, fin, log_match, row_bins, col_bins):
    p = pl.program_id(0)
    me = lax.axis_index("row")
    local, depth = rowdesc.shape[1:]
    cols = log_match.shape[2]
    na_i, nb_i = counts[pairs[p, 0]], counts[pairs[p, 1]]
    line = jnp.ones((1, LANES), jnp.float32)
    log_norm = -jnp.log(line * (na_i + nb_i).astype(jnp.float32))[:, :1]
    bin_value = bin_score[0]
    col_pot = fin[0, :, :cols]
    col_bin = fin[0, :, cols : cols + 1]
    row_bin = fin[0, :, cols + LANES : cols + LANES + 1]
    flat_pot = fin[0, :, cols + 2 * LANES :]
    wide = lax.broadcasted_iota(jnp.int32, (1, cols), 1) < nb_i
    row_index = me * local + lax.broadcasted_iota(jnp.int32, (1, local), 1)
    row_bins[pl.ds(p, 1), :] = jnp.where(row_index < na_i, bin_value + flat_pot + col_bin - log_norm, 0.0)
    col_bins[pl.ds(p, 1), :] = jnp.where(wide, bin_value + row_bin + col_pot - log_norm, 0.0)
    eye = lax.broadcasted_iota(jnp.int32, (LANES, LANES), 0) == lax.broadcasted_iota(jnp.int32, (LANES, LANES), 1)
    tops = []
    for i in range(local // LANES):
        piece = flat_pot[:, i * LANES : (i + 1) * LANES]
        tops.append(jnp.sum(jnp.where(eye, piece, 0.0), axis=1, keepdims=True))
    row_pot = jnp.concatenate(tops, axis=0)
    tall = me * local + lax.broadcasted_iota(jnp.int32, (local, 1), 0) < na_i
    flat = image.reshape(cols, depth)
    chunk = 512 if cols % 512 == 0 else LANES
    block = rowdesc[0]
    for n in range(cols // chunk):
        at = slice(n * chunk, (n + 1) * chunk)
        scores = lax.dot_general(block, flat[at, :], NT, preferred_element_type=jnp.float32) * (depth ** -0.5)
        value = scores + row_pot + col_pot[:, at] - log_norm
        log_match[0, :, at] = jnp.where(tall & wide[:, at], value, 0.0)


def on_device(teams, size, descriptors, counts, pairs, bin_score):
    images, local, depth = descriptors.shape
    cols = local * teams * size
    width = cols + 2 * LANES + local
    vmem = pl.BlockSpec(memory_space=pltpu.VMEM)
    smem = pl.BlockSpec(memory_space=pltpu.SMEM)
    f32, bf16 = jnp.float32, jnp.bfloat16
    dma = pltpu.SemaphoreType.DMA
    imgs, fin = pl.pallas_call(
        functools.partial(sinkhorn_kernel, teams, size),
        out_shape=(
            jax.ShapeDtypeStruct((teams, teams, size, local, depth), bf16),
            jax.ShapeDtypeStruct((teams, 1, width), f32),
        ),
        in_specs=[smem, smem, smem, vmem],
        out_specs=(pl.BlockSpec(memory_space=pl.ANY), vmem),
        scratch_shapes=[
            pltpu.VMEM((teams, local, depth), bf16),
            pltpu.VMEM((teams, local, depth), bf16),
            pltpu.VMEM((teams, size, local, depth), bf16),
            pltpu.VMEM((teams, size, local, depth), bf16),
            pltpu.VMEM((local, cols), f32),
            pltpu.VMEM((cols, cols), f32),
            pltpu.VMEM((cols, LANES), f32),
            pltpu.VMEM((cols, LANES), f32),
            pltpu.VMEM((cols, LANES), f32),
            pltpu.VMEM((cols, LANES), f32),
            pltpu.VMEM((cols, LANES), f32),
            pltpu.VMEM((8, cols), f32),
            pltpu.VMEM((8, LANES), f32),
            pltpu.VMEM((1, LANES), f32),
            pltpu.VMEM((teams, 1, width), f32),
            dma((2, teams)),
            dma((2, teams)),
            dma((2, teams, size)),
            dma((2, teams, size)),
            dma((teams, teams)),
            dma((teams, teams)),
            dma((teams, teams, size)),
            dma((teams, teams, size)),
            dma((teams,)),
            dma((teams,)),
            dma((teams,)),
        ],
        compiler_params=pltpu.CompilerParams(
            collective_id=0, has_side_effects=True, vmem_limit_bytes=48 * 1024 * 1024
        ),
    )(counts, pairs, bin_score, descriptors)
    return pl.pallas_call(
        functools.partial(finish_kernel, size),
        out_shape=(
            jax.ShapeDtypeStruct((teams, local, cols), f32),
            jax.ShapeDtypeStruct((teams, local), f32),
            jax.ShapeDtypeStruct((teams, cols), f32),
        ),
        grid_spec=pltpu.PrefetchScalarGridSpec(
            num_scalar_prefetch=3,
            grid=(teams,),
            in_specs=[
                pl.BlockSpec((1, local, depth), lambda p, c, q, b: (q[p, 0], 0, 0)),
                pl.BlockSpec((1, teams, size, local, depth), lambda p, c, q, b: (p, 0, 0, 0, 0)),
                pl.BlockSpec((1, 1, width), lambda p, c, q, b: (p, 0, 0)),
            ],
            out_specs=(
                pl.BlockSpec((1, local, cols), lambda p, c, q, b: (p, 0, 0)),
                pl.BlockSpec((teams, local), lambda p, c, q, b: (0, 0)),
                pl.BlockSpec((teams, cols), lambda p, c, q, b: (0, 0)),
            ),
        ),
    )(counts, pairs, bin_score, descriptors, imgs, fin)


def solution(mesh):
    group = mesh.shape["row"]

    def body(descriptors, counts, pairs, bin_score):
        teams = pairs.shape[0]
        return on_device(teams, group // teams, descriptors, counts, pairs, bin_score)

    return jax.shard_map(
        body,
        mesh=mesh,
        in_specs=(P("pair", "row", None), P("pair"), P("pair", None), P()),
        out_specs=(P("pair", "row", None), P("pair", "row"), P("pair", None)),
        check_vma=False,
    )
```

time: 122 us -> 99.9 us (0.82); the launches traced: 122 us -> 98.1 us
  Pallas kernels: 115 us -> 91.6 us
    pallas_call x1, Pallas kernels: 107 us -> 83.7 us  [on_device(): pl.pallas_call(functools.partial(sinkhorn_kernel, teams, size), out_shape...]
where the time goes in v2:
time: 99.9 us; the launch traced here: 98.1 us
  Pallas kernels  91.6 us (92%)
  local copies, waits for them, and re-layouts  5.19 us (5%)
  between operations  1.3 us (1%)
    pallas_call x1, Pallas kernels, on_device(): pl.pallas_call(functools.partial(sinkhorn_kernel, teams, size), out_shape...  83.7 us
    pallas_call x1, Pallas kernels, on_device(): pl.pallas_call(functools.partial(finish_kernel, size), out_shape=(jax.Sha...  7.84 us
    unnamed x11, local copies, waits for them, and re-layouts  5.19 us

profile of v2, /device:TPU:0, one launch (start us, length us, event | category | flops | bytes accessed | tf_op | source)
XLA Modules:
  0.0 98.1 jit_solution(5316993547656352983)
XLA Ops:
  1.3 0.8 copy.8.pairs
  2.0 0.0 copy-start.1
  2.0 1.2 %copy-done.1 = bf16[8,256,256]{2,1,0:T(8,128)(2,1)S(1)} copy-done((bf16[8,256,256]{2,1,0:T(8,128)(2,1)S(1)}, bf16[8,256,256]{2,1,0:T(8,128)(2,1)}, u32[]{:S(2)}) %copy-start.1) | copy-done | bytes 1048600
  3.3 0.0 copy-start.4
  3.3 0.7 copy-done.4
  3.9 0.0 copy-start.3
  3.9 83.7 %shard_map.67 = (bf16[4,4,2,256,256]{4,3,2,1,0:T(8,128)(2,1)S(1)}, f32[4,1,2560]{2,1,0:T(1,128)S(1)}) custom-call(s32[8]{0:T(128)S(1)} %copy-done.4, s32[4,2]{1,0:T(4,128)S(1)} %copy.8.pairs, f32[1]{0:T(128)S(6)} %copy.9.bin_score, bf16[8,256,256]{2,1,0:T(8,128)(2,1)S(1)} %copy-done.1), custom_call_target="tpu_custom_call" | custom-call | tf_op jit(solution)/shard_map/pallas_call | solution.py:325
  87.7 0.0 copy-start
  87.7 1.9 %copy-done = bf16[4,4,2,256,256]{4,3,2,1,0:T(8,128)(2,1)} copy-done((bf16[4,4,2,256,256]{4,3,2,1,0:T(8,128)(2,1)}, bf16[4,4,2,256,256]{4,3,2,1,0:T(8,128)(2,1)S(1)}, u32[]{:S(2)}) %copy-start) | copy-done | bytes 4194328
  89.6 0.0 copy-start.2
  89.6 0.6 copy-done.2
  90.2 0.0 copy-done.3
  90.2 7.8 %shard_map.68 = (f32[4,256,2048]{2,1,0:T(8,128)}, f32[4,256]{1,0:T(4,128)}, f32[4,2048]{1,0:T(4,128)}) custom-call(s32[8]{0:T(128)} %counts.3, s32[4,2]{1,0:T(4,128)} %copy-done.3, f32[1]{0:T(128)S(6)} %copy.9.bin_score, bf16[8,256,256]{2,1,0:T(8,128)(2,1)} %rowdesc.1, bf16[4,4,2,256,256]{4,3,2,1,0:T(8,128)(2,1)} %copy-done, f32[4,1,2560]{2,1,0:T(1,128)} %copy-done.2), custom_call_target="tpu_custom_call" | custom-call | tf_op jit(solution)/shard_map/pallas_call | solution.py:365
Async XLA Ops:
  2.0 1.2 %copy-start.1 = (bf16[8,256,256]{2,1,0:T(8,128)(2,1)S(1)}, bf16[8,256,256]{2,1,0:T(8,128)(2,1)}, u32[]{:S(2)}) copy-start(bf16[8,256,256]{2,1,0:T(8,128)(2,1)} %rowdesc.1) | copy-start | bytes 3145732
  3.3 0.7 copy-start.4
  3.9 86.3 %copy-start.3 = (s32[4,2]{1,0:T(4,128)}, s32[4,2]{1,0:T(4,128)S(1)}, u32[]{:S(2)}) copy-start(s32[4,2]{1,0:T(4,128)S(1)} %copy.8.pairs) | copy-start | bytes 100
  87.7 1.9 %copy-start = (bf16[4,4,2,256,256]{4,3,2,1,0:T(8,128)(2,1)}, bf16[4,4,2,256,256]{4,3,2,1,0:T(8,128)(2,1)S(1)}, u32[]{:S(2)}) copy-start(bf16[4,4,2,256,256]{4,3,2,1,0:T(8,128)(2,1)S(1)} %get-tuple-element.5.image) | copy-start | bytes 12582916
  89.6 0.6 copy-start.2

commit v3 on v2

--- a/solution.py
+++ b/solution.py
@@ -16,9 +16,9 @@
 
 
 def sinkhorn_kernel(
-    teams, size, counts, pairs, bin_score, desc, imgs, fin,
-    rowsel, colsel, rows, own, score, kern, peak, kbin, mass, left, part, b8, bbin, abin, fin_send,
-    crit_send, crit_recv, fwd_send, fwd_recv, bulk_send, bulk_recv, side_send, side_recv, fin_ssem, fin_rsem, local_sem,
+    teams, size, counts, pairs, bin_score, source_desc, imgs, fin,
+    desc, rowsel, colsel, rows, own, score, kern, peak, kbin, mass, left, part, b8, bbin, abin, fin_send,
+    crit_send, crit_recv, fwd_send, fwd_recv, bulk_send, bulk_recv, side_send, side_recv, fin_ssem, fin_rsem, local_sem, load_sem,
 ):
     me = lax.axis_index("row")
     team, member = me // size, me % size
@@ -34,12 +34,15 @@
             src_ref=src, dst_ref=dst, send_sem=ssem, recv_sem=rsem, device_id=device(t, m), device_id_type=MESH
         )
 
+    load = pltpu.make_async_copy(source_desc, desc, load_sem)
+    load.start()
     barrier = pltpu.get_barrier_semaphore()
     for dz in range(1, teams):
         pl.semaphore_signal(barrier, inc=1, device_id=device((team + dz) % teams, member), device_id_type=MESH)
     for d in range(1, size):
         pl.semaphore_signal(barrier, inc=1, device_id=device(team, (member + d) % size), device_id_type=MESH)
 
+    load.wait()
     for p in range(teams):
         colsel[p] = desc[pairs[p, 1]]
         rowsel[p] = desc[pairs[p, 0]]
@@ -328,9 +331,10 @@
             jax.ShapeDtypeStruct((teams, teams, size, local, depth), bf16),
             jax.ShapeDtypeStruct((teams, 1, width), f32),
         ),
-        in_specs=[smem, smem, smem, vmem],
+        in_specs=[smem, smem, smem, pl.BlockSpec(memory_space=pl.ANY)],
         out_specs=(pl.BlockSpec(memory_space=pl.ANY), vmem),
         scratch_shapes=[
+            pltpu.VMEM((images, local, depth), bf16),
             pltpu.VMEM((teams, local, depth), bf16),
             pltpu.VMEM((teams, local, depth), bf16),
             pltpu.VMEM((teams, size, local, depth), bf16),
@@ -357,9 +361,10 @@
             dma((teams,)),
             dma((teams,)),
             dma((teams,)),
+            dma,
         ],
         compiler_params=pltpu.CompilerParams(
-            collective_id=0, has_side_effects=True, vmem_limit_bytes=48 * 1024 * 1024
+            collective_id=0, has_side_effects=True, vmem_limit_bytes=60 * 1024 * 1024
         ),
     )(counts, pairs, bin_score, descriptors)
     return pl.pallas_call(

time: 99.9 us -> 96.7 us (0.968); the launches traced: 98.1 us -> 96.3 us
  local copies, waits for them, and re-layouts: 5.19 us -> 1.34 us
  Pallas kernels: 91.6 us -> 93.7 us
    unnamed x11 -> x1, local copies, waits for them, and re-layouts: 5.19 us -> 1.34 us
    pallas_call x1, Pallas kernels: 83.7 us -> 85.9 us  [on_device(): pl.pallas_call(functools.partial(sinkhorn_kernel, teams, size), out_shape...]
where the time goes in v3:
time: 96.7 us; the launch traced here: 96.3 us
  Pallas kernels  93.7 us (97%)
  local copies, waits for them, and re-layouts  1.34 us (1%)
  between operations  1.29 us (1%)
    pallas_call x1, Pallas kernels, on_device(): pl.pallas_call(functools.partial(sinkhorn_kernel, teams, size), out_shape...  85.9 us
    pallas_call x1, Pallas kernels, on_device(): pl.pallas_call(functools.partial(finish_kernel, size), out_shape=(jax.Sha...  7.78 us

profile of v3, /device:TPU:0, one launch (start us, length us, event | category | flops | bytes accessed | tf_op | source)
XLA Modules:
  0.0 96.3 jit_solution(6725013895706525872)
XLA Ops:
  1.3 1.3 %copy.8.pairs = s32[4,2]{1,0:T(4,128)} copy(s32[4,2]{0,1:T(2,128)} %param.6) | data formatting | bytes 64 | tf_op args[2]
  2.6 85.9 %shard_map.67 = (bf16[4,4,2,256,256]{4,3,2,1,0:T(8,128)(2,1)}, f32[4,1,2560]{2,1,0:T(1,128)}) custom-call(s32[8]{0:T(128)} %counts.3, s32[4,2]{1,0:T(4,128)} %copy.8.pairs, f32[1]{0:T(128)S(6)} %copy.9.bin_score, bf16[8,256,256]{2,1,0:T(8,128)(2,1)} %rowdesc.1), custom_call_target="tpu_custom_call" | custom-call | tf_op jit(solution)/shard_map/pallas_call | solution.py:328
  88.5 7.8 %shard_map.68 = (f32[4,256,2048]{2,1,0:T(8,128)}, f32[4,256]{1,0:T(4,128)}, f32[4,2048]{1,0:T(4,128)}) custom-call(s32[8]{0:T(128)} %counts.3, s32[4,2]{1,0:T(4,128)} %copy.8.pairs, f32[1]{0:T(128)S(6)} %copy.9.bin_score, bf16[8,256,256]{2,1,0:T(8,128)(2,1)} %rowdesc.1, bf16[4,4,2,256,256]{4,3,2,1,0:T(8,128)(2,1)} %get-tuple-element.5.image, ...), custom_call_target="tpu_custom_call" | custom-call | tf_op jit(solution)/shard_map/pallas_call | solution.py:370
